TPU v7x, 8 devices: a whole 2x2x1 slice. The times are simulated.
8 devices in a mesh: dp: 1 (over z), z: 2 (over y), y: 2 (over x), x: 2 (over core).
Axes of the slice: x: 2, y: 2, z: 1, core: 2. Of those that a mesh axis runs over, the one named last changes fastest.
Arguments:
- volume: bfloat16 [64, 48, 48, 48], P('dp', 'x', 'y', 'z')
- kernels: bfloat16 [3, 64, 64, 3, 3, 3], replicated
- biases: float32 [3, 64], replicated
Outputs:
- output: bfloat16 [64, 48, 48, 48], P('dp', 'x', 'y', 'z')
All inputs are finite; a program needn't handle non-finite values.
Results may differ from a plain program's by a relative error of at most 0.001.
Values are sent between devices in bfloat16 or wider.
A program may use at most 1 GiB of HBM per device.

v0:
```python
import jax
import jax.numpy as jnp
from jax import lax
from jax.sharding import PartitionSpec as P

VOL_DIMS = (("x", 1), ("y", 2), ("z", 3))


def solution(mesh):
    def exchange(local_block, axis_name, array_dim, halo_width):
        axis_count = mesh.shape[axis_name]
        extent = local_block.shape[array_dim]
        low_planes = lax.slice_in_dim(local_block, 0, halo_width, axis=array_dim)
        high_planes = lax.slice_in_dim(local_block, extent - halo_width, extent, axis=array_dim)
        if axis_count == 1:
            from_lower = jnp.zeros_like(high_planes)
            from_upper = jnp.zeros_like(low_planes)
        else:
            from_lower = lax.ppermute(high_planes, axis_name, [(source, source + 1) for source in range(axis_count - 1)])
            from_upper = lax.ppermute(low_planes, axis_name, [(source + 1, source) for source in range(axis_count - 1)])
        return jnp.concatenate([from_lower, local_block, from_upper], axis=array_dim)

    def local_layers(local_block, kernels, biases):
        halo_width = kernels.shape[3] // 2
        current = local_block
        for layer_idx in range(kernels.shape[0]):
            padded = current
            for axis_name, array_dim in VOL_DIMS:
                padded = exchange(padded, axis_name, array_dim, halo_width)
            conv_out = lax.conv_general_dilated(padded[None], kernels[layer_idx], (1, 1, 1), "VALID", dimension_numbers=("NCDHW", "OIDHW", "NCDHW"), preferred_element_type=jnp.float32)[0]
            activated = jax.nn.gelu(conv_out + biases[layer_idx][:, None, None, None])
            current = (current.astype(jnp.float32) + activated).astype(jnp.bfloat16)
        return current

    vol_spec = P("dp", "x", "y", "z")
    return jax.shard_map(local_layers, mesh=mesh, in_specs=(vol_spec, P(), P()), out_specs=vol_spec, check_vma=False)
```

profile of v0, /device:TPU:0, one launch (start us, length us, event | category | flops | bytes accessed | tf_op | source)
XLA Modules:
  0.0 299.1 jit_solution(14996123257303926313)
XLA Ops:
  1.0 2.8 collective-permute-start
  3.8 1.3 collective-permute-start.1
  5.1 2.8 constant_dynamic-update-slice_fusion.1
  8.1 4.2 %collective-permute-start.2 = (bf16[64,26,1,24]{0,3,2,1:T(8,128)(2,1)S(1)}, bf16[64,26,1,24]{0,3,2,1:T(8,128)(2,1)S(1)}, u32[]{:S(2)}, u32[]{:S(2)}) collective-permute-start(bf16[64,26,1,24]{0,3,2,1:T(8,128)(2,1)S(1)} %get-tuple-element.15), channel_id=1, source_target_pairs={{0,2},{1,3},{4,6},{5,7}} | collective-permute-start | bytes 239624 | tf_op jit(solution)/shard_map/ppermute | solution.py:19
  12.3 1.3 collective-permute-start.3
  13.6 3.0 %collective-permute-done.2 = bf16[64,26,1,24]{0,3,2,1:T(8,128)(2,1)S(1)} collective-permute-done((bf16[64,26,1,24]{0,3,2,1:T(8,128)(2,1)S(1)}, bf16[64,26,1,24]{0,3,2,1:T(8,128)(2,1)S(1)}, u32[]{:S(2)}, u32[]{:S(2)}) %collective-permute-start.2) | collective-permute-done | bytes 79904 | tf_op jit(solution)/shard_map/ppermute | solution.py:19
  16.6 4.5 %collective-permute-done.3 = bf16[64,26,1,24]{0,3,2,1:T(8,128)(2,1)S(1)} collective-permute-done((bf16[64,26,1,24]{0,3,2,1:T(8,128)(2,1)S(1)}, bf16[64,26,1,24]{0,3,2,1:T(8,128)(2,1)S(1)}, u32[]{:S(2)}, u32[]{:S(2)}) %collective-permute-start.3) | collective-permute-done | bytes 79904 | tf_op jit(solution)/shard_map/ppermute | solution.py:20
  21.9 3.4 %collective-permute-start.4 = (bf16[64,26,26,1]{0,3,2,1:T(2,128)(2,1)S(1)}, bf16[64,26,26,1]{0,3,2,1:T(2,128)(2,1)S(1)}, u32[]{:S(2)}, u32[]{:S(2)}) collective-permute-start(bf16[64,26,26,1]{0,3,2,1:T(2,128)(2,1)S(1)} %get-tuple-element.9), channel_id=1, source_target_pairs={{0,4},{1,5},{2,6},{3,7}} | collective-permute-start | bytes 259592 | tf_op jit(solution)/shard_map/ppermute | solution.py:19
  25.3 1.3 collective-permute-start.5
  27.1 5.6 %collective-permute-done.4 = bf16[64,26,26,1]{0,3,2,1:T(2,128)(2,1)S(1)} collective-permute-done((bf16[64,26,26,1]{0,3,2,1:T(2,128)(2,1)S(1)}, bf16[64,26,26,1]{0,3,2,1:T(2,128)(2,1)S(1)}, u32[]{:S(2)}, u32[]{:S(2)}) %collective-permute-start.4) | collective-permute-done | bytes 86560 | tf_op jit(solution)/shard_map/ppermute | solution.py:19
  32.8 4.2 %collective-permute-done.5 = bf16[64,26,26,1]{0,3,2,1:T(2,128)(2,1)S(1)} collective-permute-done((bf16[64,26,26,1]{0,3,2,1:T(2,128)(2,1)S(1)}, bf16[64,26,26,1]{0,3,2,1:T(2,128)(2,1)S(1)}, u32[]{:S(2)}, u32[]{:S(2)}) %collective-permute-start.5) | collective-permute-done | bytes 86560 | tf_op jit(solution)/shard_map/ppermute | solution.py:20
  36.9 4.1 %maximum_bitcast_fusion = bf16[64,26,26,1,26]{0,4,2,1,3:T(8,128)(2,1)S(1)} fusion(bf16[64,26,26,1]{0,3,2,1:T(2,128)(2,1)S(1)} %collective-permute-done.5, bf16[64,26,1,24]{0,3,2,1:T(8,128)(2,1)S(1)} %collective-permute-done.3, bf16[64,26,24,24]{0,3,2,1:T(8,128)(2,1)S(1)} %constant_dynamic-update-slice_fusion, ...), kind=kLoop, calls=%fused_computation.58 | loop fusion | flops 11248640 | bytes 4499456 | tf_op jit(solution)/shard_map/broadcast_in_dim | solution.py:30
  41.0 1.5 pad
  44.5 38.9 %broadcast_select_fusion.2 = f32[24,24,8,4,64]{4,2,3,1,0:T(8,128)} fusion(pred[8,4]{0,1:T(4,128)(4,1)S(1)} %copy-done.3, bf16[64,26,26,1,7,2]{0,4,5,2,1,3:T(8,128)(2,1)S(1)} %slice.104, bf16[64,26,26,1,8,4]{0,4,5,2,1,3:T(8,128)(2,1)S(1)} %copy.6, bf16[3,64,64,3,3,3]{2,1,5,4,3,0:T(8,128)(2,1)} %param.4), kind=kOutput, calls=%fused_computation.63 | convolution fusion | flops 4090503168 | bytes 9141280 | tf_op jit(solution)/shard_map/conv_general_dilated | solution.py:30
  83.4 11.9 %copy.7 = f32[24,24,8,4,64]{4,1,3,2,0:T(8,128)S(1)} copy(f32[24,24,8,4,64]{4,2,3,1,0:T(8,128)} %broadcast_select_fusion.2) | data formatting | bytes 9437184 | tf_op jit(solution)/shard_map/conv_general_dilated | solution.py:30
  95.4 2.8 fusion.32
  98.2 1.3 collective-permute-start.6
  99.6 1.3 collective-permute-start.7
  100.9 2.0 collective-permute-done.7
  103.5 1.4 collective-permute-start.8
  104.9 1.3 collective-permute-start.9
  106.2 5.9 %collective-permute-done.8 = bf16[64,26,1,24]{0,2,3,1:T(2,128)(2,1)S(1)} collective-permute-done((bf16[64,26,1,24]{0,2,3,1:T(2,128)(2,1)S(1)}, bf16[64,26,1,24]{0,2,3,1:T(2,128)(2,1)S(1)}, u32[]{:S(2)}, u32[]{:S(2)}) %collective-permute-start.8) | collective-permute-done | bytes 79904 | tf_op jit(solution)/shard_map/ppermute | solution.py:19
  112.1 4.2 %collective-permute-done.9 = bf16[64,26,1,24]{0,2,3,1:T(2,128)(2,1)S(1)} collective-permute-done((bf16[64,26,1,24]{0,2,3,1:T(2,128)(2,1)S(1)}, bf16[64,26,1,24]{0,2,3,1:T(2,128)(2,1)S(1)}, u32[]{:S(2)}, u32[]{:S(2)}) %collective-permute-start.9) | collective-permute-done | bytes 79904 | tf_op jit(solution)/shard_map/ppermute | solution.py:20
  116.5 1.4 collective-permute-start.10
  119.2 2.6 collective-permute-done.10
  121.9 4.1 %collective-permute-done.11 = bf16[64,26,26,1]{0,2,3,1:T(8,128)(2,1)S(1)} collective-permute-done((bf16[64,26,26,1]{0,2,3,1:T(8,128)(2,1)S(1)}, bf16[64,26,26,1]{0,2,3,1:T(8,128)(2,1)S(1)}, u32[]{:S(2)}, u32[]{:S(2)}) %collective-permute-start.11) | collective-permute-done | bytes 86560 | tf_op jit(solution)/shard_map/ppermute | solution.py:20
  126.0 8.3 %maximum_bitcast_fusion.1 = bf16[64,26,26,1,26]{0,2,4,1,3:T(8,128)(2,1)} fusion(bf16[64,26,26,1]{0,2,3,1:T(8,128)(2,1)S(1)} %collective-permute-done.11, bf16[64,26,1,24]{0,2,3,1:T(2,128)(2,1)S(1)} %collective-permute-done.9, bf16[64,1,24,24]{0,2,3,1:T(8,128)(2,1)S(1)} %collective-permute-done.7, bf16[64,24,24,24]{0,2,3,1:T(8,128)(2,1)S(1)} %fusion.32, ...), kind=kLoop, calls=%fused_computation.59 | loop fusion | flops 15748096 | bytes 4499456 | tf_op jit(solution)/shard_map/broadcast_in_dim | solution.py:30
  134.3 4.3 %pad.2 = bf16[64,26,26,1,32]{0,2,4,1,3:T(8,128)(2,1)S(1)} pad(bf16[64,26,26,1,26]{0,2,4,1,3:T(8,128)(2,1)} %maximum_bitcast_fusion.1, bf16[]{:T(256)} %constant.8), padding=0_0x0_0x0_0x0_0x0_6 | pad | bytes 5018626 | tf_op jit(solution)/shard_map/broadcast_in_dim | solution.py:30
  138.6 5.1 %copy.10 = bf16[64,26,26,1,8,4]{0,4,5,2,1,3:T(8,128)(2,1)S(1)} copy(bf16[64,26,26,1,8,4]{0,2,5,4,1,3:T(8,128)(2,1)S(1)} %bitcast.70) | data formatting | bytes 5537792 | tf_op jit(solution)/shard_map/conv_general_dilated | solution.py:30
  144.5 38.9 %broadcast_select_fusion.1 = f32[24,24,8,4,64]{4,2,3,1,0:T(8,128)} fusion(pred[8,4]{0,1:T(4,128)(4,1)S(1)} %copy-done.3, bf16[64,26,26,1,7,2]{0,4,5,2,1,3:T(8,128)(2,1)S(1)} %slice.108, bf16[64,26,26,1,8,4]{0,4,5,2,1,3:T(8,128)(2,1)S(1)} %copy.10, bf16[3,64,64,3,3,3]{2,1,5,4,3,0:T(8,128)(2,1)} %param.4), kind=kOutput, calls=%fused_computation.62 | convolution fusion | flops 4090503168 | bytes 9141280 | tf_op jit(solution)/shard_map/conv_general_dilated | solution.py:30
  183.4 11.8 %copy.11 = f32[24,24,8,4,64]{4,1,3,2,0:T(8,128)S(1)} copy(f32[24,24,8,4,64]{4,2,3,1,0:T(8,128)} %broadcast_select_fusion.1) | data formatting | bytes 9437184 | tf_op jit(solution)/shard_map/conv_general_dilated | solution.py:30
  195.2 3.0 %fusion.41 = bf16[64,24,24,24]{0,2,3,1:T(8,128)(2,1)S(1)} fusion(f32[24,24,1,32,64]{4,1,3,0,2:T(8,128)S(1)} %bitcast.67, bf16[64,24,24,24]{0,2,3,1:T(8,128)(2,1)S(1)} %fusion.32, f32[64]{0:T(128)S(1)} %get-tuple-element.25), kind=kLoop, calls=%fused_computation.42 | loop fusion | flops 10616832 | bytes 7078144 | tf_op jit(solution)/shard_map/convert_element_type | solution.py:32
  198.3 1.3 collective-permute-start.12
  200.9 2.0 collective-permute-done.13
  203.5 1.4 collective-permute-start.14
  205.0 1.3 collective-permute-start.15
  206.3 5.9 %collective-permute-done.14 = bf16[64,26,1,24]{0,2,3,1:T(2,128)(2,1)S(1)} collective-permute-done((bf16[64,26,1,24]{0,2,3,1:T(2,128)(2,1)S(1)}, bf16[64,26,1,24]{0,2,3,1:T(2,128)(2,1)S(1)}, u32[]{:S(2)}, u32[]{:S(2)}) %collective-permute-start.14) | collective-permute-done | bytes 79904 | tf_op jit(solution)/shard_map/ppermute | solution.py:19
  212.2 4.2 %collective-permute-done.15 = bf16[64,26,1,24]{0,2,3,1:T(2,128)(2,1)S(1)} collective-permute-done((bf16[64,26,1,24]{0,2,3,1:T(2,128)(2,1)S(1)}, bf16[64,26,1,24]{0,2,3,1:T(2,128)(2,1)S(1)}, u32[]{:S(2)}, u32[]{:S(2)}) %collective-permute-start.15) | collective-permute-done | bytes 79904 | tf_op jit(solution)/shard_map/ppermute | solution.py:20
  216.5 1.4 collective-permute-start.16
  219.3 2.6 collective-permute-done.16
  221.9 4.1 %collective-permute-done.17 = bf16[64,26,26,1]{0,2,3,1:T(8,128)(2,1)S(1)} collective-permute-done((bf16[64,26,26,1]{0,2,3,1:T(8,128)(2,1)S(1)}, bf16[64,26,26,1]{0,2,3,1:T(8,128)(2,1)S(1)}, u32[]{:S(2)}, u32[]{:S(2)}) %collective-permute-start.17) | collective-permute-done | bytes 86560 | tf_op jit(solution)/shard_map/ppermute | solution.py:20
  226.0 8.8 %maximum_bitcast_fusion.2 = bf16[64,26,26,1,26]{0,2,4,1,3:T(8,128)(2,1)S(1)} fusion(bf16[64,26,26,1]{0,2,3,1:T(8,128)(2,1)S(1)} %collective-permute-done.17, bf16[64,26,1,24]{0,2,3,1:T(2,128)(2,1)S(1)} %collective-permute-done.15, bf16[64,1,24,24]{0,2,3,1:T(8,128)(2,1)S(1)} %collective-permute-done.13, bf16[64,24,24,24]{0,2,3,1:T(8,128)(2,1)S(1)} %fusion.41, ...), kind=kLoop, calls=%fused_computation.60 | loop fusion | flops 15748096 | bytes 4499456 | tf_op jit(solution)/shard_map/broadcast_in_dim | solution.py:30
  234.9 1.8 pad.4
  236.7 5.1 %copy.14 = bf16[64,26,26,1,8,4]{0,4,5,2,1,3:T(8,128)(2,1)S(1)} copy(bf16[64,26,26,1,8,4]{0,2,5,4,1,3:T(8,128)(2,1)S(1)} %bitcast.69) | data formatting | bytes 5537792 | tf_op jit(solution)/shard_map/conv_general_dilated | solution.py:30
  242.6 38.8 %broadcast_select_fusion = f32[24,24,8,4,64]{4,2,3,1,0:T(8,128)} fusion(pred[8,4]{0,1:T(4,128)(4,1)S(1)} %copy-done.3, bf16[64,26,26,1,7,2]{0,4,5,2,1,3:T(8,128)(2,1)S(1)} %slice.112, bf16[64,26,26,1,8,4]{0,4,5,2,1,3:T(8,128)(2,1)S(1)} %copy.14, bf16[3,64,64,3,3,3]{2,1,5,4,3,0:T(8,128)(2,1)} %param.4), kind=kOutput, calls=%fused_computation.61 | convolution fusion | flops 4090503168 | bytes 9141280 | tf_op jit(solution)/shard_map/conv_general_dilated | solution.py:30
  281.4 11.8 %copy.15 = f32[24,24,8,4,64]{4,1,3,2,0:T(8,128)S(1)} copy(f32[24,24,8,4,64]{4,2,3,1,0:T(8,128)} %broadcast_select_fusion) | data formatting | bytes 9437184 | tf_op jit(solution)/shard_map/conv_general_dilated | solution.py:30
  293.2 3.0 %fusion.50 = bf16[64,24,24,24]{0,2,3,1:T(8,128)(2,1)S(1)} fusion(f32[24,24,1,32,64]{4,1,3,0,2:T(8,128)S(1)} %bitcast.66, bf16[64,24,24,24]{0,2,3,1:T(8,128)(2,1)S(1)} %fusion.41, f32[64]{0:T(128)S(1)} %copy-done.1), kind=kLoop, calls=%fused_computation.51 | loop fusion | flops 10616832 | bytes 7078144 | tf_op jit(solution)/shard_map/convert_element_type | solution.py:32
  296.2 2.5 copy.16
  (31 shorter events, 11.5 us)
Async XLA Ops:
  0.0 26.6 %copy-start.2 = (f32[3,64]{1,0:T(4,128)S(1)}, f32[3,64]{1,0:T(4,128)}, u32[]{:S(2)}) copy-start(f32[3,64]{1,0:T(4,128)} %param.5) | copy-start | bytes 2308
  1.0 4.1 %collective-permute-start = (bf16[64,1,24,24]{0,3,2,1:T(8,128)(2,1)S(1)}, bf16[64,1,24,24]{0,3,2,1:T(8,128)(2,1)S(1)}, u32[]{:S(2)}, u32[]{:S(2)}) collective-permute-start(bf16[64,1,24,24]{0,3,2,1:T(8,128)(2,1)S(1)} %get-tuple-element.22), channel_id=1, source_target_pairs={{0,1},{2,3},{4,5},{6,7}} | collective-permute-start | bytes 221192 | tf_op jit(solution)/shard_map/ppermute | solution.py:19
  3.8 4.2 %collective-permute-start.1 = (bf16[64,1,24,24]{0,3,2,1:T(8,128)(2,1)S(1)}, bf16[64,1,24,24]{0,3,2,1:T(8,128)(2,1)S(1)}, u32[]{:S(2)}, u32[]{:S(2)}) collective-permute-start(bf16[64,1,24,24]{0,3,2,1:T(8,128)(2,1)S(1)} %get-tuple-element.21), channel_id=1, source_target_pairs={{1,0},{3,2},{5,4},{7,6}} | collective-permute-start | bytes 221192 | tf_op jit(solution)/shard_map/ppermute | solution.py:20
  8.1 8.5 %collective-permute-start.2 = (bf16[64,26,1,24]{0,3,2,1:T(8,128)(2,1)S(1)}, bf16[64,26,1,24]{0,3,2,1:T(8,128)(2,1)S(1)}, u32[]{:S(2)}, u32[]{:S(2)}) collective-permute-start(bf16[64,26,1,24]{0,3,2,1:T(8,128)(2,1)S(1)} %get-tuple-element.15), channel_id=1, source_target_pairs={{0,2},{1,3},{4,6},{5,7}} | collective-permute-start | bytes 239624 | tf_op jit(solution)/shard_map/ppermute | solution.py:19
  12.3 8.8 %collective-permute-start.3 = (bf16[64,26,1,24]{0,3,2,1:T(8,128)(2,1)S(1)}, bf16[64,26,1,24]{0,3,2,1:T(8,128)(2,1)S(1)}, u32[]{:S(2)}, u32[]{:S(2)}) collective-permute-start(bf16[64,26,1,24]{0,3,2,1:T(8,128)(2,1)S(1)} %get-tuple-element.16), channel_id=1, source_target_pairs={{2,0},{3,1},{6,4},{7,5}} | collective-permute-start | bytes 239624 | tf_op jit(solution)/shard_map/ppermute | solution.py:20
  21.9 10.9 %collective-permute-start.4 = (bf16[64,26,26,1]{0,3,2,1:T(2,128)(2,1)S(1)}, bf16[64,26,26,1]{0,3,2,1:T(2,128)(2,1)S(1)}, u32[]{:S(2)}, u32[]{:S(2)}) collective-permute-start(bf16[64,26,26,1]{0,3,2,1:T(2,128)(2,1)S(1)} %get-tuple-element.9), channel_id=1, source_target_pairs={{0,4},{1,5},{2,6},{3,7}} | collective-permute-start | bytes 259592 | tf_op jit(solution)/shard_map/ppermute | solution.py:19
  25.3 11.6 %collective-permute-start.5 = (bf16[64,26,26,1]{0,3,2,1:T(2,128)(2,1)S(1)}, bf16[64,26,26,1]{0,3,2,1:T(2,128)(2,1)S(1)}, u32[]{:S(2)}, u32[]{:S(2)}) collective-permute-start(bf16[64,26,26,1]{0,3,2,1:T(2,128)(2,1)S(1)} %get-tuple-element.10), channel_id=1, source_target_pairs={{4,0},{5,1},{6,2},{7,3}} | collective-permute-start | bytes 259592 | tf_op jit(solution)/shard_map/ppermute | solution.py:20
  42.5 2.0 copy-start.3
  83.4 12.0 %copy-start = (bf16[64,24,24,24]{0,3,2,1:T(8,128)(2,1)S(1)}, bf16[64,24,24,24]{0,3,2,1:T(8,128)(2,1)}, u32[]{:S(2)}) copy-start(bf16[64,24,24,24]{0,3,2,1:T(8,128)(2,1)} %param.3) | copy-start | bytes 5308420
  98.2 2.6 collective-permute-start.6
  99.6 3.3 %collective-permute-start.7 = (bf16[64,1,24,24]{0,2,3,1:T(8,128)(2,1)S(1)}, bf16[64,1,24,24]{0,2,3,1:T(8,128)(2,1)S(1)}, u32[]{:S(2)}, u32[]{:S(2)}) collective-permute-start(bf16[64,1,24,24]{0,2,3,1:T(8,128)(2,1)S(1)} %get-tuple-element.20), channel_id=1, source_target_pairs={{1,0},{3,2},{5,4},{7,6}} | collective-permute-start | bytes 221192 | tf_op jit(solution)/shard_map/ppermute | solution.py:20
  103.5 8.6 %collective-permute-start.8 = (bf16[64,26,1,24]{0,2,3,1:T(2,128)(2,1)S(1)}, bf16[64,26,1,24]{0,2,3,1:T(2,128)(2,1)S(1)}, u32[]{:S(2)}, u32[]{:S(2)}) collective-permute-start(bf16[64,26,1,24]{0,2,3,1:T(2,128)(2,1)S(1)} %get-tuple-element.13), channel_id=1, source_target_pairs={{0,2},{1,3},{4,6},{5,7}} | collective-permute-start | bytes 239624 | tf_op jit(solution)/shard_map/ppermute | solution.py:19
  104.9 11.3 %collective-permute-start.9 = (bf16[64,26,1,24]{0,2,3,1:T(2,128)(2,1)S(1)}, bf16[64,26,1,24]{0,2,3,1:T(2,128)(2,1)S(1)}, u32[]{:S(2)}, u32[]{:S(2)}) collective-permute-start(bf16[64,26,1,24]{0,2,3,1:T(2,128)(2,1)S(1)} %get-tuple-element.14), channel_id=1, source_target_pairs={{2,0},{3,1},{6,4},{7,5}} | collective-permute-start | bytes 239624 | tf_op jit(solution)/shard_map/ppermute | solution.py:20
  116.5 5.4 %collective-permute-start.10 = (bf16[64,26,26,1]{0,2,3,1:T(8,128)(2,1)S(1)}, bf16[64,26,26,1]{0,2,3,1:T(8,128)(2,1)S(1)}, u32[]{:S(2)}, u32[]{:S(2)}) collective-permute-start(bf16[64,26,26,1]{0,2,3,1:T(8,128)(2,1)S(1)} %get-tuple-element.7), channel_id=1, source_target_pairs={{0,4},{1,5},{2,6},{3,7}} | collective-permute-start | bytes 259592 | tf_op jit(solution)/shard_map/ppermute | solution.py:19
  117.9 8.1 %collective-permute-start.11 = (bf16[64,26,26,1]{0,2,3,1:T(8,128)(2,1)S(1)}, bf16[64,26,26,1]{0,2,3,1:T(8,128)(2,1)S(1)}, u32[]{:S(2)}, u32[]{:S(2)}) collective-permute-start(bf16[64,26,26,1]{0,2,3,1:T(8,128)(2,1)S(1)} %get-tuple-element.8), channel_id=1, source_target_pairs={{4,0},{5,1},{6,2},{7,3}} | collective-permute-start | bytes 259592 | tf_op jit(solution)/shard_map/ppermute | solution.py:20
  198.3 2.6 collective-permute-start.12
  199.6 3.3 %collective-permute-start.13 = (bf16[64,1,24,24]{0,2,3,1:T(8,128)(2,1)S(1)}, bf16[64,1,24,24]{0,2,3,1:T(8,128)(2,1)S(1)}, u32[]{:S(2)}, u32[]{:S(2)}) collective-permute-start(bf16[64,1,24,24]{0,2,3,1:T(8,128)(2,1)S(1)} %get-tuple-element.18), channel_id=1, source_target_pairs={{1,0},{3,2},{5,4},{7,6}} | collective-permute-start | bytes 221192 | tf_op jit(solution)/shard_map/ppermute | solution.py:20
  203.5 8.6 %collective-permute-start.14 = (bf16[64,26,1,24]{0,2,3,1:T(2,128)(2,1)S(1)}, bf16[64,26,1,24]{0,2,3,1:T(2,128)(2,1)S(1)}, u32[]{:S(2)}, u32[]{:S(2)}) collective-permute-start(bf16[64,26,1,24]{0,2,3,1:T(2,128)(2,1)S(1)} %get-tuple-element.11), channel_id=1, source_target_pairs={{0,2},{1,3},{4,6},{5,7}} | collective-permute-start | bytes 239624 | tf_op jit(solution)/shard_map/ppermute | solution.py:19
  205.0 11.3 %collective-permute-start.15 = (bf16[64,26,1,24]{0,2,3,1:T(2,128)(2,1)S(1)}, bf16[64,26,1,24]{0,2,3,1:T(2,128)(2,1)S(1)}, u32[]{:S(2)}, u32[]{:S(2)}) collective-permute-start(bf16[64,26,1,24]{0,2,3,1:T(2,128)(2,1)S(1)} %get-tuple-element.12), channel_id=1, source_target_pairs={{2,0},{3,1},{6,4},{7,5}} | collective-permute-start | bytes 239624 | tf_op jit(solution)/shard_map/ppermute | solution.py:20
  216.5 5.4 %collective-permute-start.16 = (bf16[64,26,26,1]{0,2,3,1:T(8,128)(2,1)S(1)}, bf16[64,26,26,1]{0,2,3,1:T(8,128)(2,1)S(1)}, u32[]{:S(2)}, u32[]{:S(2)}) collective-permute-start(bf16[64,26,26,1]{0,2,3,1:T(8,128)(2,1)S(1)} %get-tuple-element.5), channel_id=1, source_target_pairs={{0,4},{1,5},{2,6},{3,7}} | collective-permute-start | bytes 259592 | tf_op jit(solution)/shard_map/ppermute | solution.py:19
  218.0 8.1 %collective-permute-start.17 = (bf16[64,26,26,1]{0,2,3,1:T(8,128)(2,1)S(1)}, bf16[64,26,26,1]{0,2,3,1:T(8,128)(2,1)S(1)}, u32[]{:S(2)}, u32[]{:S(2)}) collective-permute-start(bf16[64,26,26,1]{0,2,3,1:T(8,128)(2,1)S(1)} %get-tuple-element.6), channel_id=1, source_target_pairs={{4,0},{5,1},{6,2},{7,3}} | collective-permute-start | bytes 259592 | tf_op jit(solution)/shard_map/ppermute | solution.py:20
  281.4 11.8 %copy-start.1 = (f32[64]{0:T(128)S(1)}, f32[64]{0:T(128)}, u32[]{:S(2)}) copy-start(f32[64]{0:T(128)} %get-tuple-element.23) | copy-start | bytes 772
where the time goes:
time: 305 us; the launch traced here: 299 us
  matrix products  117 us (38%)
  local copies, waits for them, and re-layouts  63.9 us (21%)
  waiting for transfers between devices  54.8 us (18%)
  other arithmetic  32.5 us (11%)
  starting transfers between devices  30.4 us (10%)
    conv_general_dilated x3, matrix products, local_layers(): lax.conv_general_dilated(padded[None], kernels[layer_idx], (1, 1, 1), 'VA...  117 us
    conv_general_dilated x9, local copies, waits for them, and re-layouts, local_layers(): lax.conv_general_dilated(padded[None], kernels[layer_idx], (1, 1, 1), 'VA...  49.1 us
    ppermute x9, waiting for transfers between devices, exchange(): lax.ppermute(low_planes, axis_name, [(source + 1, source) for source in r...  29.1 us
    ppermute x9, waiting for transfers between devices, exchange(): lax.ppermute(high_planes, axis_name, [(source, source + 1) for source in...  25.7 us
    broadcast_in_dim x3, other arithmetic, local_layers(): padded[None]  21.1 us
    ppermute x9, starting transfers between devices, exchange(): lax.ppermute(high_planes, axis_name, [(source, source + 1) for source in...  18.8 us
    ppermute x9, starting transfers between devices, exchange(): lax.ppermute(low_planes, axis_name, [(source + 1, source) for source in r...  11.6 us
    convert_element_type x3, other arithmetic, local_layers(): current = (current.astype(jnp.float32) + activated).astype(jnp.bfloat16)  8.86 us
  transfers between devices with their start and end apart: 18, of which 14 were waited for; matrix products, arithmetic and copies ran while one was open for 1% of the time, Pallas kernels for 0%

commit v1 on v0

v1 whole, which is shorter than its diff:
```python
import jax
import jax.numpy as jnp
from jax import lax
from jax.experimental import pallas as pl
from jax.experimental.pallas import tpu as pltpu
from jax.sharding import PartitionSpec as P

LAYERS, CH, TAPS, N = 3, 64, 9, 24
PAIRS = N // 2
SLABS = PAIRS + 1
PITCH, Z0 = 40, 8
GROUPS = ((1, 2), (3, 4), (5, 6), (7, 8), (9, 10), (11, 12))
SEND_LAG = 4
CHUNK = 2
WAIT_AHEAD = 1
F32, BF16 = jnp.float32, jnp.bfloat16


def kernel(vol, g_hbm, bias, out, v0, v1, v2, b_ref, io, g_v, wt, zsend, zrecv, crn,
           in_sem, g_sem, out_sem, send_sem, recv_sem):
    v = (v0, v1, v2)
    ix, iy, iz = lax.axis_index("x"), lax.axis_index("y"), lax.axis_index("z")

    def peer(*axes):
        mine = {"x": ix, "y": iy, "z": iz}
        return {a: 1 - mine[a] for a in axes}

    barrier = pltpu.get_barrier_semaphore()
    all_peers = (("x",), ("y",), ("z",), ("x", "y"), ("x", "z"), ("y", "z"), ("x", "y", "z"))
    for axes in all_peers:
        pl.semaphore_signal(barrier, inc=1, device_id=peer(*axes), device_id_type=pl.DeviceIdType.MESH)

    def plane0(j0, j1):
        return 2 * (ix * (j0 - 1) + (1 - ix) * (PAIRS - j1))

    def in_copy(i):
        j0, j1 = GROUPS[i]
        planes = pl.ds(plane0(j0, j1), 2 * (j1 - j0 + 1))
        return pltpu.make_async_copy(vol.at[planes], io.at[planes], in_sem.at[i])

    def out_copy(i):
        j0, j1 = GROUPS[i]
        planes = pl.ds(plane0(j0, j1), 2 * (j1 - j0 + 1))
        return pltpu.make_async_copy(io.at[planes], out.at[planes], out_sem.at[i])

    def g_copy(l):
        return pltpu.make_async_copy(g_hbm.at[l], g_v.at[l], g_sem.at[l])

    for i in range(len(GROUPS)):
        in_copy(i).start()
    for l in range(LAYERS):
        g_copy(l).start()

    def clear(j, carry):
        for l in range(LAYERS):
            v[l][j, 25 * iy, Z0:Z0 + N, :] = jnp.zeros((N, 128), F32)
        return carry

    lax.fori_loop(0, SLABS, clear, 0)

    y_src, y_dst = 1 + 23 * (1 - iy), 25 * iy
    kinds = 3 * len(GROUPS) + 4

    def remote(l, slot, src, dst, *axes):
        return pltpu.make_async_remote_copy(
            src_ref=src, dst_ref=dst, send_sem=send_sem.at[l * kinds + slot], recv_sem=recv_sem.at[l * kinds + slot],
            device_id=peer(*axes), device_id_type=pl.DeviceIdType.MESH)

    def copies(l, i):
        j0, j1 = GROUPS[i]
        slabs, rows, tile = pl.ds(j0, j1 - j0 + 1), pl.ds(Z0, N), pl.ds(16 * (1 - iy), 8)
        got = [
            remote(l, 3 * i, v[l].at[slabs, y_src, rows], v[l].at[slabs, y_dst, rows], "y"),
            remote(l, 3 * i + 1, zsend.at[l, slabs], zrecv.at[l, slabs], "z"),
            remote(l, 3 * i + 2, zsend.at[l, slabs, tile], crn.at[l, slabs], "y", "z"),
        ]
        if i == 0:
            n = 3 * len(GROUPS)
            got += [
                remote(l, n, v[l].at[1, pl.ds(1, N), rows], v[l].at[0, pl.ds(1, N), rows], "x"),
                remote(l, n + 1, v[l].at[1, y_src, rows], v[l].at[0, y_dst, rows], "x", "y"),
                remote(l, n + 2, zsend.at[l, 1], zrecv.at[l, 0], "x", "z"),
                remote(l, n + 3, zsend.at[l, 1, tile], crn.at[l, 0], "x", "y", "z"),
            ]
        return got

    def stage(l, j):
        lo, hi = v[l][j, 1:N + 1, Z0, :], v[l][j, 1:N + 1, Z0 + N - 1, :]
        zsend[l, j] = jnp.where(iz == 0, hi, lo)

    def send(l, i):
        j0, j1 = GROUPS[i]
        for j in range(j0, j1 + 1):
            stage(l, j)
        for c in copies(l, i):
            c.start()

    def fix(l, j):
        r, zero = zrecv[l, j], jnp.zeros((N, 128), F32)
        v[l][j, 1:N + 1, Z0 - 1, :] = jnp.where(iz == 1, r, zero)
        v[l][j, 1:N + 1, Z0 + N, :] = jnp.where(iz == 0, r, zero)
        for block, row, side in ((0, 7, 1), (25, 0, 0)):
            r = jnp.where(iy == side, crn[l, j, row:row + 1, :], zero[:1])
            v[l][j, block, Z0 - 1:Z0, :] = jnp.where(iz == 1, r, zero[:1])
            v[l][j, block, Z0 + N:Z0 + N + 1, :] = jnp.where(iz == 0, r, zero[:1])

    def receive(l, i):
        for c in copies(l, i):
            c.wait_recv()
        if i == 0:
            fix(l, 0)
        j0, j1 = GROUPS[i]
        for j in range(j0, j1 + 1):
            fix(l, j)

    def load_slab(j, carry):
        x = plane0(j, j)
        for y in range(0, N, 4):
            a, b = io[x, y:y + 4].astype(F32), io[x + 1, y:y + 4].astype(F32)
            v0[j, y + 1:y + 5, Z0:Z0 + N, :] = jnp.concatenate([a, b], axis=2)
        return carry

    def weights(l, carry):
        g_copy(l).wait()
        zero = jnp.zeros((CH, CH), F32)
        for t in range(TAPS):
            e, s = t // 3, t % 3
            ga, gb, gc = (g_v[l, a, e, s].astype(F32) for a in range(3))
            rows = (jnp.concatenate([gb, gc], axis=1), jnp.concatenate([ga, gb], axis=1),
                    jnp.concatenate([zero, ga], axis=1), jnp.concatenate([gc, zero], axis=1))
            for slot in range(4):
                wt[l, CH * slot:CH * slot + CH, 128 * t:128 * t + 128] = rows[slot]
        return carry

    prev = (lax.broadcasted_iota(jnp.int32, (CHUNK, N, 128), 2) < CH).astype(jnp.int32) == ix

    def finish(l, j):
        row = bias[l:l + 1, :]
        row = jnp.concatenate([row, row], axis=1).reshape(1, 1, 128)
        x = plane0(j, j)
        for y in range(0, N, CHUNK):
            ys = slice(y, y + CHUNK)
            blocks = slice(y + 1, y + 1 + CHUNK)
            after = b_ref[j + 1, ys, :, 128:] if j < PAIRS else jnp.zeros((CHUNK, N, 128), F32)
            acc = b_ref[j, ys, :, :128] + jnp.where(prev, b_ref[j - 1, ys, :, 128:], after) + row
            half = 0.5 * acc
            act = half + half * jnp.tanh(acc * (0.7978845608028654 + 0.035677408136300125 * (acc * acc)))
            new = v[l][j, blocks, Z0:Z0 + N, :] + act
            if l + 1 < LAYERS:
                v[l + 1][j, blocks, Z0:Z0 + N, :] = new.astype(BF16).astype(F32)
            else:
                io[x, ys] = new[:, :, :CH].astype(BF16)
                io[x + 1, ys] = pltpu.roll(new, CH, 2)[:, :, :CH].astype(BF16)

    def multiply(n):
        l, j = divmod(n, SLABS)
        parts = [v[l][j, t // 3:t // 3 + N, Z0 - 1 + t % 3:Z0 - 1 + t % 3 + N, :].reshape(N * N, 128) for t in range(TAPS)]
        prod = lax.dot_general(jnp.concatenate(parts, axis=1), wt[l], (((1,), (1,)), ((), ())), preferred_element_type=F32)
        b_ref[j] = prod.reshape(N, N, 256)

    pl.semaphore_wait(barrier, len(all_peers))
    for i, (j0, j1) in enumerate(GROUPS):
        in_copy(i).wait()
        lax.fori_loop(j0, j1 + 1, load_slab, 0)
        send(0, i)
    lax.fori_loop(0, LAYERS, weights, 0)

    last = LAYERS * SLABS
    for n in range(last + 4):
        for i, (j0, j1) in enumerate(GROUPS):
            for l in range(LAYERS):
                if n == max(0, l * SLABS + (j0 if i else 0) - WAIT_AHEAD):
                    receive(l, i)
                if n == l * SLABS + j1 + SEND_LAG and l + 1 < LAYERS:
                    send(l + 1, i)
            if n == (LAYERS - 1) * SLABS + j1 + 3:
                out_copy(i).start()
        if n < last:
            multiply(n)
        if 2 <= n <= last + 1 and (n - 2) % SLABS:
            finish(*divmod(n - 2, SLABS))
    for l in range(LAYERS):
        for i in range(len(GROUPS)):
            for c in copies(l, i):
                c.wait_send()
    for i in range(len(GROUPS)):
        out_copy(i).wait()


def solution(mesh):
    any_spec, vmem = pl.BlockSpec(memory_space=pl.ANY), pl.BlockSpec(memory_space=pltpu.VMEM)
    copies = LAYERS * (3 * len(GROUPS) + 4)

    def local(block, kernels, biases):
        vol = jnp.transpose(block, (1, 2, 3, 0))
        g = jnp.transpose(kernels, (0, 3, 4, 5, 1, 2))
        out = pl.pallas_call(
            kernel,
            out_shape=jax.ShapeDtypeStruct((N, N, N, CH), BF16),
            in_specs=[any_spec, any_spec, vmem],
            out_specs=any_spec,
            scratch_shapes=[pltpu.VMEM((SLABS, 26, PITCH, 128), F32)] * 3 + [
                pltpu.VMEM((SLABS, N, N, 256), F32),
                pltpu.VMEM((N, N, N, CH), BF16),
                pltpu.VMEM((LAYERS, 3, 3, 3, CH, CH), BF16),
                pltpu.VMEM((LAYERS, 256, 128 * TAPS), F32),
                pltpu.VMEM((LAYERS, SLABS, N, 128), F32),
                pltpu.VMEM((LAYERS, SLABS, N, 128), F32),
                pltpu.VMEM((LAYERS, SLABS, 8, 128), F32),
                pltpu.SemaphoreType.DMA((len(GROUPS),)),
                pltpu.SemaphoreType.DMA((LAYERS,)),
                pltpu.SemaphoreType.DMA((len(GROUPS),)),
                pltpu.SemaphoreType.DMA((copies,)),
                pltpu.SemaphoreType.DMA((copies,)),
            ],
            compiler_params=pltpu.CompilerParams(collective_id=0, has_side_effects=True, vmem_limit_bytes=60 * 2 ** 20),
        )(vol, g, biases)
        return jnp.transpose(out, (3, 0, 1, 2))

    spec = P("dp", "x", "y", "z")
    return jax.shard_map(local, mesh=mesh, in_specs=(spec, P(), P()), out_specs=spec, check_vma=False)
```

time: 305 us -> 39.1 us (0.13); the launches traced: 299 us -> 39 us
  matrix products: 117 us -> 0 us
  local copies, waits for them, and re-layouts: 63.9 us -> 4.4 us
  waiting for transfers between devices: 54.8 us -> 0 us
  Pallas kernels: 0 us -> 34.6 us
  other arithmetic: 32.5 us -> 0 us
  starting transfers between devices: 30.4 us -> 0 us
    conv_general_dilated x3 -> x0, matrix products: 117 us -> none  [local_layers(): lax.conv_general_dilated(padded[None], kernels[layer_idx], (1, 1, 1), 'VA...]
    ppermute x18 -> x0, waiting for transfers between devices: 54.8 us -> none  [the longest x9 29.1 us: exchange(): lax.ppermute(low_planes, axis_name, [(source + 1, source) for source in r...]
    conv_general_dilated x9 -> x0, local copies, waits for them, and re-layouts: 49.1 us -> none  [local_layers(): lax.conv_general_dilated(padded[None], kernels[layer_idx], (1, 1, 1), 'VA...]
    pallas_call x0 -> x1, Pallas kernels: none -> 34.6 us  [local(): pl.pallas_call(kernel, out_shape=jax.ShapeDtypeStruct((N, N, N, CH), BF16...]
    ppermute x18 -> x0, starting transfers between devices: 30.4 us -> none  [the longest x9 18.8 us: exchange(): lax.ppermute(high_planes, axis_name, [(source, source + 1) for source in...]
    broadcast_in_dim x3 -> x0, other arithmetic: 21.1 us -> none  [local_layers(): padded[None]]
    convert_element_type x3 -> x0, other arithmetic: 8.86 us -> none  [local_layers(): current = (current.astype(jnp.float32) + activated).astype(jnp.bfloat16)]
    broadcast_in_dim x3 -> x0, local copies, waits for them, and re-layouts: 7.71 us -> none  [local_layers(): padded[None]]
  transfers between devices with their start and end apart: 18 -> 0, of which waited for: 14 -> 0; matrix products, arithmetic and copies ran while one was open for 1% -> 0% of each run, Pallas kernels for 0% -> 0%
where the time goes in v1:
time: 39.1 us; the launch traced here: 39 us
  Pallas kernels  34.6 us (88%)
  local copies, waits for them, and re-layouts  4.4 us (11%)
    pallas_call x1, Pallas kernels, local(): pl.pallas_call(kernel, out_shape=jax.ShapeDtypeStruct((N, N, N, CH), BF16...  34.6 us
    unnamed x1, local copies, waits for them, and re-layouts  4.4 us

profile of v1, /device:TPU:0, one launch (start us, length us, event | category | flops | bytes accessed | tf_op | source)
XLA Modules:
  0.0 39.0 jit_solution(1953048820057718768)
XLA Ops:
  0.0 34.6 %shard_map.37 = bf16[24,24,24,64]{3,2,1,0:T(8,128)(2,1)} custom-call(bf16[24,24,24,64]{3,2,1,0:T(8,128)(2,1)} %bitcast.4, bf16[3,3,3,3,64,64]{5,4,3,2,1,0:T(8,128)(2,1)} %bitcast.5, f32[3,64]{1,0:T(4,128)} %bias.1), custom_call_target="tpu_custom_call" | custom-call | tf_op jit(solution)/shard_map/pallas_call | solution.py:197
  34.6 4.4 %copy.5 = bf16[64,24,24,24]{0,3,2,1:T(8,128)(2,1)} copy(bf16[64,24,24,24]{0,3,2,1:T(8,128)(2,1)} %bitcast.3) | data formatting | bytes 3538944

commit v2 on v1

v2 whole, which is shorter than its diff:
```python
import jax
import jax.numpy as jnp
from jax import lax
from jax.experimental import pallas as pl
from jax.experimental.pallas import tpu as pltpu
from jax.sharding import PartitionSpec as P

LAYERS, CH, TAPS, N = 3, 64, 9, 24
PAIRS = N // 2
SLABS = PAIRS + 1
PITCH, Z0 = 40, 8
ORDER = (1, 2, 3, 0, 4, 5, 6, 7, 8, 9, 10, 11, 12)
LOADS = ((1, 1), (2, 3), (4, 6), (7, 9), (10, 12))
FENCES = (1, 3, 5, 7, 9, 11)
CHUNK = 2
F32, BF16 = jnp.float32, jnp.bfloat16

PLACE = {j: p for p, j in enumerate(ORDER)}
READY = {j: max(PLACE[k] for k in (j - 1, j, j + 1) if k in PLACE) + 1 for j in range(1, SLABS)}
POINTS = [SLABS * l + p for l in range(-1, 2) for p in FENCES]


def _groups():
    found = {}
    for j in range(1, SLABS):
        key = (min(p for p in POINTS if p > READY[j]), max(p for p in POINTS if p <= SLABS + PLACE[j]))
        found.setdefault(key, []).append(j)
    return [(min(js), max(js), start, end) for (start, end), js in sorted(found.items(), key=lambda kv: kv[1])]


GROUPS = _groups()
X_END = max(p for p in POINTS if p <= SLABS + PLACE[0])


def kernel(vol, g_hbm, bias_hbm, out, v0, v1, v2, b_ref, io, g_v, wt, zsend, zrecv, ysend, yrecv, xsend, xrecv,
           csend, crecv, bias, in_sem, bias_sem, g_sem, send_sem, recv_sem):
    v = (v0, v1, v2)
    ip, ib, iz = lax.axis_index("y"), lax.axis_index("x"), lax.axis_index("z")

    def peer(*axes):
        mine = {"y": ip, "x": ib, "z": iz}
        return {a: 1 - mine[a] for a in axes}

    barrier = pltpu.get_barrier_semaphore()
    all_peers = (("x",), ("y",), ("z",), ("x", "y"), ("x", "z"), ("y", "z"), ("x", "y", "z"))
    for axes in all_peers:
        pl.semaphore_signal(barrier, inc=1, device_id=peer(*axes), device_id_type=pl.DeviceIdType.MESH)

    def plane0(j0, j1):
        return 2 * (ip * (j0 - 1) + (1 - ip) * (PAIRS - j1))

    def in_copy(i):
        j0, j1 = LOADS[i]
        planes = pl.ds(plane0(j0, j1), 2 * (j1 - j0 + 1))
        return pltpu.make_async_copy(vol.at[:, planes], io.at[:, planes], in_sem.at[i])

    def g_copy(l):
        return pltpu.make_async_copy(g_hbm.at[l], g_v.at[l], g_sem.at[l])

    for i in range(len(LOADS)):
        in_copy(i).start()
    for l in range(LAYERS):
        g_copy(l).start()
    bias_copy = pltpu.make_async_copy(bias_hbm, bias, bias_sem)
    bias_copy.start()

    y_src = 1 + (N - 1) * (1 - ib)
    kinds = 3 * len(GROUPS) + 4

    def remote(l, slot, src, dst, *axes):
        return pltpu.make_async_remote_copy(
            src_ref=src, dst_ref=dst, send_sem=send_sem.at[l * kinds + slot], recv_sem=recv_sem.at[l * kinds + slot],
            device_id=peer(*axes), device_id_type=pl.DeviceIdType.MESH)

    def copies(l, i):
        j0, j1 = GROUPS[i][:2]
        slabs = pl.ds(j0, j1 - j0 + 1)
        got = [
            remote(l, 3 * i, ysend.at[l, slabs], yrecv.at[l, slabs], "x"),
            remote(l, 3 * i + 1, zsend.at[l, slabs], zrecv.at[l, slabs], "z"),
            remote(l, 3 * i + 2, csend.at[l, slabs], crecv.at[l, slabs], "x", "z"),
        ]
        if i == 0:
            n = 3 * len(GROUPS)
            got += [
                remote(l, n, xsend.at[l], xrecv.at[l], "y"),
                remote(l, n + 1, ysend.at[l, 1], yrecv.at[l, 0], "x", "y"),
                remote(l, n + 2, zsend.at[l, 1], zrecv.at[l, 0], "y", "z"),
                remote(l, n + 3, csend.at[l, 1], crecv.at[l, 0], "x", "y", "z"),
            ]
        return got

    near = (lax.broadcasted_iota(jnp.int32, (N // 2, N, 128), 2) < CH).astype(jnp.int32) == ip

    def stage(l, j):
        lo, hi = v[l][j, 1:N + 1, Z0, :], v[l][j, 1:N + 1, Z0 + N - 1, :]
        edge = jnp.where(iz == 0, hi, lo)
        zsend[l, j] = edge.astype(BF16)
        ysend[l, j] = v[l][j, y_src, Z0:Z0 + N, :].astype(BF16)
        csend[l, j, 0:1] = jnp.where(ib == 0, edge[N - 1:N], edge[0:1])
        if j == 1:
            half = N // 2
            a, b = v[l][1, 1:half + 1, Z0:Z0 + N, :], v[l][1, half + 1:N + 1, Z0:Z0 + N, :]
            stay, move = jnp.where(ip == 1, a, b), jnp.where(ip == 1, b, a)
            xsend[l] = jnp.where(near, stay, pltpu.roll(move, CH, 2)).astype(BF16)

    def send(l, i):
        j0, j1 = GROUPS[i][:2]
        for j in range(j0, j1 + 1):
            stage(l, j)
        for c in copies(l, i):
            c.start()

    def fix(l, j):
        zero = jnp.zeros((N, 128), F32)
        r = zrecv[l, j].astype(F32)
        v[l][j, 1:N + 1, Z0 - 1, :] = jnp.where(iz == 1, r, zero)
        v[l][j, 1:N + 1, Z0 + N, :] = jnp.where(iz == 0, r, zero)
        r, c = yrecv[l, j].astype(F32), crecv[l, j, 0:1, :]
        for block, side in ((0, 1), (N + 1, 0)):
            v[l][j, block, Z0:Z0 + N, :] = jnp.where(ib == side, r, zero)
            corner = jnp.where(ib == side, c, zero[:1])
            v[l][j, block, Z0 - 1:Z0, :] = jnp.where(iz == 1, corner, zero[:1])
            v[l][j, block, Z0 + N:Z0 + N + 1, :] = jnp.where(iz == 0, corner, zero[:1])
        if j == 0:
            half = N // 2
            r = xrecv[l].astype(F32)
            t = pltpu.roll(r, CH, 2)
            v[l][0, 1:half + 1, Z0:Z0 + N, :] = jnp.where(ip == 0, r, t)
            v[l][0, half + 1:N + 1, Z0:Z0 + N, :] = jnp.where(ip == 0, t, r)

    def receive(l, i):
        for c in copies(l, i)[:3]:
            c.wait_recv()
        j0, j1 = GROUPS[i][:2]
        for j in range(j0, j1 + 1):
            fix(l, j)

    def receive_x(l):
        for c in copies(l, 0)[3:]:
            c.wait_recv()
        fix(l, 0)

    def load_slab(j, carry):
        x = plane0(j, j)
        for y in range(0, N, 4):
            a, b = io[y:y + 4, x].astype(F32), io[y:y + 4, x + 1].astype(F32)
            v0[j, y + 1:y + 5, Z0:Z0 + N, :] = jnp.concatenate([a, b], axis=2)
        return carry

    def weights(l, carry):
        g_copy(l).wait()
        zero = jnp.zeros((CH, CH), F32)
        for t in range(TAPS):
            e, s = t // 3, t % 3
            ga, gb, gc = (g_v[l, e, a, s].astype(F32) for a in range(3))
            rows = (jnp.concatenate([gb, gc], axis=1), jnp.concatenate([ga, gb], axis=1),
                    jnp.concatenate([zero, ga], axis=1), jnp.concatenate([gc, zero], axis=1))
            for slot in range(4):
                wt[l, CH * slot:CH * slot + CH, 128 * t:128 * t + 128] = rows[slot]
        return carry

    prev = (lax.broadcasted_iota(jnp.int32, (CHUNK, N, 128), 2) < CH).astype(jnp.int32) == ip

    def finish(l, j):
        row = bias[l:l + 1, :]
        row = jnp.concatenate([row, row], axis=1).reshape(1, 1, 128)
        x = plane0(j, j)
        for y in range(0, N, CHUNK):
            ys = slice(y, y + CHUNK)
            blocks = slice(y + 1, y + 1 + CHUNK)
            after = b_ref[j + 1, ys, :, 128:] if j < PAIRS else jnp.zeros((CHUNK, N, 128), F32)
            acc = b_ref[j, ys, :, :128] + jnp.where(prev, b_ref[j - 1, ys, :, 128:], after) + row
            half = 0.5 * acc
            act = half + half * jnp.tanh(acc * (0.7978845608028654 + 0.035677408136300125 * (acc * acc)))
            new = v[l][j, blocks, Z0:Z0 + N, :] + act
            if l + 1 < LAYERS:
                v[l + 1][j, blocks, Z0:Z0 + N, :] = new.astype(BF16).astype(F32)
            else:
                out[ys, x] = new[:, :, :CH].astype(BF16)
                out[ys, x + 1] = pltpu.roll(new, CH, 2)[:, :, :CH].astype(BF16)

    def multiply(l, j):
        parts = [v[l][j, t // 3:t // 3 + N, Z0 - 1 + t % 3:Z0 - 1 + t % 3 + N, :].reshape(N * N, 128) for t in range(TAPS)]
        prod = lax.dot_general(jnp.concatenate(parts, axis=1), wt[l], (((1,), (1,)), ((), ())), preferred_element_type=F32)
        b_ref[j] = prod.reshape(N, N, 256)

    pl.semaphore_wait(barrier, len(all_peers))
    done = 0
    for i, (j0, j1) in enumerate(LOADS):
        in_copy(i).wait()
        lax.fori_loop(j0, j1 + 1, load_slab, 0)
        while done < len(GROUPS) and GROUPS[done][1] <= j1:
            send(0, done)
            done += 1
    lax.fori_loop(0, LAYERS, weights, 0)
    bias_copy.wait()

    for n in range(LAYERS * SLABS + 2):
        for l in range(1, LAYERS):
            for i, (_, _, start, _) in enumerate(GROUPS):
                if n == (l - 1) * SLABS + start:
                    send(l, i)
        for l in range(LAYERS):
            for i, (_, _, _, end) in enumerate(GROUPS):
                if n == max(0, (l - 1) * SLABS + end):
                    receive(l, i)
            if n == max(0, (l - 1) * SLABS + X_END):
                receive_x(l)
        if n < LAYERS * SLABS:
            multiply(n // SLABS, ORDER[n % SLABS])
        for l in range(LAYERS):
            for j in range(1, SLABS):
                if n - l * SLABS == READY[j]:
                    finish(l, j)
    for l in range(LAYERS):
        for i in range(len(GROUPS)):
            for c in copies(l, i):
                c.wait_send()


def solution(mesh):
    any_spec, vmem = pl.BlockSpec(memory_space=pl.ANY), pl.BlockSpec(memory_space=pltpu.VMEM)
    copies = LAYERS * (3 * len(GROUPS) + 4)

    def local(block, kernels, biases):
        vol = jnp.transpose(block, (1, 2, 3, 0))
        g = jnp.transpose(kernels, (0, 3, 4, 5, 1, 2))
        out = pl.pallas_call(
            kernel,
            out_shape=pltpu.VMEM((N, N, N, CH), BF16),
            in_specs=[any_spec] * 3,
            out_specs=vmem,
            scratch_shapes=[pltpu.VMEM((SLABS, 26, PITCH, 128), F32)] * 3 + [
                pltpu.VMEM((SLABS, N, N, 256), F32),
                pltpu.VMEM((N, N, N, CH), BF16),
                pltpu.VMEM((LAYERS, 3, 3, 3, CH, CH), BF16),
                pltpu.VMEM((LAYERS, 256, 128 * TAPS), F32),
                pltpu.VMEM((LAYERS, SLABS, N, 128), BF16),
                pltpu.VMEM((LAYERS, SLABS, N, 128), BF16),
                pltpu.VMEM((LAYERS, SLABS, N, 128), BF16),
                pltpu.VMEM((LAYERS, SLABS, N, 128), BF16),
                pltpu.VMEM((LAYERS, N // 2, N, 128), BF16),
                pltpu.VMEM((LAYERS, N // 2, N, 128), BF16),
                pltpu.VMEM((LAYERS, SLABS, 8, 128), F32),
                pltpu.VMEM((LAYERS, SLABS, 8, 128), F32),
                pltpu.VMEM((LAYERS, CH), F32),
                pltpu.SemaphoreType.DMA((len(LOADS),)),
                pltpu.SemaphoreType.DMA,
                pltpu.SemaphoreType.DMA((LAYERS,)),
                pltpu.SemaphoreType.DMA((copies,)),
                pltpu.SemaphoreType.DMA((copies,)),
            ],
            compiler_params=pltpu.CompilerParams(collective_id=0, has_side_effects=True, vmem_limit_bytes=52 * 2 ** 20),
        )(vol, g, biases)
        return jnp.transpose(out, (3, 0, 1, 2))

    spec = P("dp", "x", "y", "z")
    return jax.shard_map(local, mesh=mesh, in_specs=(spec, P(), P()), out_specs=spec, check_vma=False)
```

time: 39.1 us -> 33.6 us (0.86)
  Pallas kernels: 34.6 us -> 31.7 us
  local copies, waits for them, and re-layouts: 4.4 us -> 1.8 us
    pallas_call x1, Pallas kernels: 34.6 us -> 31.7 us  [local(): pl.pallas_call(kernel, out_shape=pltpu.VMEM((N, N, N, CH), BF16), in_spec...]
    unnamed x1, local copies, waits for them, and re-layouts: 4.4 us -> 1.8 us
where the time goes in v2:
time: 33.6 us; the launch traced here: 33.5 us
  Pallas kernels  31.7 us (94%)
  local copies, waits for them, and re-layouts  1.8 us (5%)
    pallas_call x1, Pallas kernels, local(): pl.pallas_call(kernel, out_shape=pltpu.VMEM((N, N, N, CH), BF16), in_spec...  31.7 us
    unnamed x1, local copies, waits for them, and re-layouts  1.8 us

profile of v2, /device:TPU:0, one launch (start us, length us, event | category | flops | bytes accessed | tf_op | source)
XLA Modules:
  0.0 33.5 jit_solution(8878244319029582951)
XLA Ops:
  0.0 31.7 %shard_map.37 = bf16[24,24,24,64]{3,2,1,0:T(8,128)(2,1)S(1)} custom-call(bf16[24,24,24,64]{3,2,1,0:T(8,128)(2,1)} %bitcast.4, bf16[3,3,3,3,64,64]{5,4,3,2,1,0:T(8,128)(2,1)} %bitcast.5, f32[3,64]{1,0:T(4,128)} %bias_hbm.1), custom_call_target="tpu_custom_call" | custom-call | tf_op jit(solution)/shard_map/pallas_call | solution.py:229
  31.7 1.8 %copy.5 = bf16[64,24,24,24]{0,3,2,1:T(8,128)(2,1)} copy(bf16[64,24,24,24]{0,3,2,1:T(8,128)(2,1)S(1)} %bitcast.3) | data formatting | bytes 3538944

commit v3 on v2

--- a/solution.py
+++ b/solution.py
@@ -13,6 +13,7 @@
 LOADS = ((1, 1), (2, 3), (4, 6), (7, 9), (10, 12))
 FENCES = (1, 3, 5, 7, 9, 11)
 CHUNK = 2
+AHEAD = 0
 F32, BF16 = jnp.float32, jnp.bfloat16
 
 PLACE = {j: p for p, j in enumerate(ORDER)}
@@ -23,17 +24,18 @@
 def _groups():
     found = {}
     for j in range(1, SLABS):
-        key = (min(p for p in POINTS if p > READY[j]), max(p for p in POINTS if p <= SLABS + PLACE[j]))
+        key = (min(p for p in POINTS if p > READY[j]), max(p for p in POINTS if p <= SLABS + PLACE[j] - AHEAD))
         found.setdefault(key, []).append(j)
     return [(min(js), max(js), start, end) for (start, end), js in sorted(found.items(), key=lambda kv: kv[1])]
 
 
 GROUPS = _groups()
-X_END = max(p for p in POINTS if p <= SLABS + PLACE[0])
+X_END = max(p for p in POINTS if p <= SLABS + PLACE[0] - AHEAD)
+PART = {j: (i, j - g[0]) for i, g in enumerate(GROUPS) for j in range(g[0], g[1] + 1)}
 
 
 def kernel(vol, g_hbm, bias_hbm, out, v0, v1, v2, b_ref, io, g_v, wt, zsend, zrecv, ysend, yrecv, xsend, xrecv,
-           csend, crecv, bias, in_sem, bias_sem, g_sem, send_sem, recv_sem):
+           csend, crecv, drecv, bias, in_sem, bias_sem, g_sem, send_sem, recv_sem):
     v = (v0, v1, v2)
     ip, ib, iz = lax.axis_index("y"), lax.axis_index("x"), lax.axis_index("z")
 
@@ -64,7 +66,6 @@
     bias_copy = pltpu.make_async_copy(bias_hbm, bias, bias_sem)
     bias_copy.start()
 
-    y_src = 1 + (N - 1) * (1 - ib)
     kinds = 3 * len(GROUPS) + 4
 
     def remote(l, slot, src, dst, *axes):
@@ -78,7 +79,7 @@
         got = [
             remote(l, 3 * i, ysend.at[l, slabs], yrecv.at[l, slabs], "x"),
             remote(l, 3 * i + 1, zsend.at[l, slabs], zrecv.at[l, slabs], "z"),
-            remote(l, 3 * i + 2, csend.at[l, slabs], crecv.at[l, slabs], "x", "z"),
+            remote(l, 3 * i + 2, csend.at[l, i], crecv.at[l, i], "x", "z"),
         ]
         if i == 0:
             n = 3 * len(GROUPS)
@@ -86,7 +87,7 @@
                 remote(l, n, xsend.at[l], xrecv.at[l], "y"),
                 remote(l, n + 1, ysend.at[l, 1], yrecv.at[l, 0], "x", "y"),
                 remote(l, n + 2, zsend.at[l, 1], zrecv.at[l, 0], "y", "z"),
-                remote(l, n + 3, csend.at[l, 1], crecv.at[l, 0], "x", "y", "z"),
+                remote(l, n + 3, csend.at[l, 0], drecv.at[l], "x", "y", "z"),
             ]
         return got
 
@@ -96,8 +97,9 @@
         lo, hi = v[l][j, 1:N + 1, Z0, :], v[l][j, 1:N + 1, Z0 + N - 1, :]
         edge = jnp.where(iz == 0, hi, lo)
         zsend[l, j] = edge.astype(BF16)
-        ysend[l, j] = v[l][j, y_src, Z0:Z0 + N, :].astype(BF16)
-        csend[l, j, 0:1] = jnp.where(ib == 0, edge[N - 1:N], edge[0:1])
+        ysend[l, j] = jnp.where(ib == 0, v[l][j, N, Z0:Z0 + N, :], v[l][j, 1, Z0:Z0 + N, :]).astype(BF16)
+        i, r = PART[j]
+        csend[l, i, r:r + 1] = jnp.where(ib == 0, edge[N - 1:N], edge[0:1])
         if j == 1:
             half = N // 2
             a, b = v[l][1, 1:half + 1, Z0:Z0 + N, :], v[l][1, half + 1:N + 1, Z0:Z0 + N, :]
@@ -105,9 +107,6 @@
             xsend[l] = jnp.where(near, stay, pltpu.roll(move, CH, 2)).astype(BF16)
 
     def send(l, i):
-        j0, j1 = GROUPS[i][:2]
-        for j in range(j0, j1 + 1):
-            stage(l, j)
         for c in copies(l, i):
             c.start()
 
@@ -116,7 +115,9 @@
         r = zrecv[l, j].astype(F32)
         v[l][j, 1:N + 1, Z0 - 1, :] = jnp.where(iz == 1, r, zero)
         v[l][j, 1:N + 1, Z0 + N, :] = jnp.where(iz == 0, r, zero)
-        r, c = yrecv[l, j].astype(F32), crecv[l, j, 0:1, :]
+        r = yrecv[l, j].astype(F32)
+        i, k = PART[j] if j else (0, 0)
+        c = crecv[l, i, k:k + 1, :] if j else drecv[l, 0:1, :]
         for block, side in ((0, 1), (N + 1, 0)):
             v[l][j, block, Z0:Z0 + N, :] = jnp.where(ib == side, r, zero)
             corner = jnp.where(ib == side, c, zero[:1])
@@ -132,14 +133,10 @@
     def receive(l, i):
         for c in copies(l, i)[:3]:
             c.wait_recv()
-        j0, j1 = GROUPS[i][:2]
-        for j in range(j0, j1 + 1):
-            fix(l, j)
 
     def receive_x(l):
         for c in copies(l, 0)[3:]:
             c.wait_recv()
-        fix(l, 0)
 
     def load_slab(j, carry):
         x = plane0(j, j)
@@ -185,12 +182,15 @@
         prod = lax.dot_general(jnp.concatenate(parts, axis=1), wt[l], (((1,), (1,)), ((), ())), preferred_element_type=F32)
         b_ref[j] = prod.reshape(N, N, 256)
 
-    pl.semaphore_wait(barrier, len(all_peers))
     done = 0
     for i, (j0, j1) in enumerate(LOADS):
         in_copy(i).wait()
         lax.fori_loop(j0, j1 + 1, load_slab, 0)
         while done < len(GROUPS) and GROUPS[done][1] <= j1:
+            for j in range(GROUPS[done][0], GROUPS[done][1] + 1):
+                stage(0, j)
+            if done == 0:
+                pl.semaphore_wait(barrier, len(all_peers))
             send(0, done)
             done += 1
     lax.fori_loop(0, LAYERS, weights, 0)
@@ -201,18 +201,25 @@
             for i, (_, _, start, _) in enumerate(GROUPS):
                 if n == (l - 1) * SLABS + start:
                     send(l, i)
+        arrived = []
         for l in range(LAYERS):
-            for i, (_, _, _, end) in enumerate(GROUPS):
+            for i, (j0, j1, _, end) in enumerate(GROUPS):
                 if n == max(0, (l - 1) * SLABS + end):
                     receive(l, i)
+                    arrived += [(l, j) for j in range(j0, j1 + 1)]
             if n == max(0, (l - 1) * SLABS + X_END):
                 receive_x(l)
-        if n < LAYERS * SLABS:
-            multiply(n // SLABS, ORDER[n % SLABS])
+                arrived.append((l, 0))
         for l in range(LAYERS):
             for j in range(1, SLABS):
                 if n - l * SLABS == READY[j]:
                     finish(l, j)
+                    if l + 1 < LAYERS:
+                        stage(l + 1, j)
+        for l, j in arrived:
+            fix(l, j)
+        if n < LAYERS * SLABS:
+            multiply(n // SLABS, ORDER[n % SLABS])
     for l in range(LAYERS):
         for i in range(len(GROUPS)):
             for c in copies(l, i):
@@ -242,8 +249,9 @@
                 pltpu.VMEM((LAYERS, SLABS, N, 128), BF16),
                 pltpu.VMEM((LAYERS, N // 2, N, 128), BF16),
                 pltpu.VMEM((LAYERS, N // 2, N, 128), BF16),
-                pltpu.VMEM((LAYERS, SLABS, 8, 128), F32),
-                pltpu.VMEM((LAYERS, SLABS, 8, 128), F32),
+                pltpu.VMEM((LAYERS, len(GROUPS), 8, 128), F32),
+                pltpu.VMEM((LAYERS, len(GROUPS), 8, 128), F32),
+                pltpu.VMEM((LAYERS, 8, 128), F32),
                 pltpu.VMEM((LAYERS, CH), F32),
                 pltpu.SemaphoreType.DMA((len(LOADS),)),
                 pltpu.SemaphoreType.DMA,

time: 33.6 us -> 33.1 us (0.985)
  Pallas kernels: 31.7 us -> 31.2 us
    pallas_call x1, Pallas kernels: 31.7 us -> 31.2 us  [local(): pl.pallas_call(kernel, out_shape=pltpu.VMEM((N, N, N, CH), BF16), in_spec...]
where the time goes in v3:
time: 33.1 us; the launch traced here: 33 us
  Pallas kernels  31.2 us (94%)
  local copies, waits for them, and re-layouts  1.8 us (5%)
    pallas_call x1, Pallas kernels, local(): pl.pallas_call(kernel, out_shape=pltpu.VMEM((N, N, N, CH), BF16), in_spec...  31.2 us
    unnamed x1, local copies, waits for them, and re-layouts  1.8 us

profile of v3, /device:TPU:0, one launch (start us, length us, event | category | flops | bytes accessed | tf_op | source)
XLA Modules:
  0.0 33.0 jit_solution(14603091313608096516)
XLA Ops:
  0.0 31.2 %shard_map.37 = bf16[24,24,24,64]{3,2,1,0:T(8,128)(2,1)S(1)} custom-call(bf16[24,24,24,64]{3,2,1,0:T(8,128)(2,1)} %bitcast.4, bf16[3,3,3,3,64,64]{5,4,3,2,1,0:T(8,128)(2,1)} %bitcast.5, f32[3,64]{1,0:T(4,128)} %bias_hbm.1), custom_call_target="tpu_custom_call" | custom-call | tf_op jit(solution)/shard_map/pallas_call | solution.py:236
  31.2 1.8 %copy.5 = bf16[64,24,24,24]{0,3,2,1:T(8,128)(2,1)} copy(bf16[64,24,24,24]{0,3,2,1:T(8,128)(2,1)S(1)} %bitcast.3) | data formatting | bytes 3538944

commit v4 on v3

--- a/solution.py
+++ b/solution.py
@@ -93,8 +93,14 @@
 
     near = (lax.broadcasted_iota(jnp.int32, (N // 2, N, 128), 2) < CH).astype(jnp.int32) == ip
 
+    def flat(l):
+        return v[l].reshape(SLABS * (N + 2) * PITCH, 128)
+
+    def column(j, row):
+        return pl.ds((j * (N + 2) + 1) * PITCH + row, N, stride=PITCH)
+
     def stage(l, j):
-        lo, hi = v[l][j, 1:N + 1, Z0, :], v[l][j, 1:N + 1, Z0 + N - 1, :]
+        lo, hi = flat(l)[column(j, Z0), :], flat(l)[column(j, Z0 + N - 1), :]
         edge = jnp.where(iz == 0, hi, lo)
         zsend[l, j] = edge.astype(BF16)
         ysend[l, j] = jnp.where(ib == 0, v[l][j, N, Z0:Z0 + N, :], v[l][j, 1, Z0:Z0 + N, :]).astype(BF16)
@@ -113,8 +119,8 @@
     def fix(l, j):
         zero = jnp.zeros((N, 128), F32)
         r = zrecv[l, j].astype(F32)
-        v[l][j, 1:N + 1, Z0 - 1, :] = jnp.where(iz == 1, r, zero)
-        v[l][j, 1:N + 1, Z0 + N, :] = jnp.where(iz == 0, r, zero)
+        flat(l)[column(j, Z0 - 1), :] = jnp.where(iz == 1, r, zero)
+        flat(l)[column(j, Z0 + N), :] = jnp.where(iz == 0, r, zero)
         r = yrecv[l, j].astype(F32)
         i, k = PART[j] if j else (0, 0)
         c = crecv[l, i, k:k + 1, :] if j else drecv[l, 0:1, :]

time: 33.1 us -> 32.5 us (0.982)
  Pallas kernels: 31.2 us -> 30.6 us
    pallas_call x1, Pallas kernels: 31.2 us -> 30.6 us  [local(): pl.pallas_call(kernel, out_shape=pltpu.VMEM((N, N, N, CH), BF16), in_spec...]
where the time goes in v4:
time: 32.5 us; the launch traced here: 32.4 us
  Pallas kernels  30.6 us (94%)
  local copies, waits for them, and re-layouts  1.8 us (6%)
    pallas_call x1, Pallas kernels, local(): pl.pallas_call(kernel, out_shape=pltpu.VMEM((N, N, N, CH), BF16), in_spec...  30.6 us
    unnamed x1, local copies, waits for them, and re-layouts  1.8 us

profile of v4, /device:TPU:0, one launch (start us, length us, event | category | flops | bytes accessed | tf_op | source)
XLA Modules:
  0.0 32.4 jit_solution(7751404422946597160)
XLA Ops:
  0.0 30.6 %shard_map.37 = bf16[24,24,24,64]{3,2,1,0:T(8,128)(2,1)S(1)} custom-call(bf16[24,24,24,64]{3,2,1,0:T(8,128)(2,1)} %bitcast.4, bf16[3,3,3,3,64,64]{5,4,3,2,1,0:T(8,128)(2,1)} %bitcast.5, f32[3,64]{1,0:T(4,128)} %bias_hbm.1), custom_call_target="tpu_custom_call" | custom-call | tf_op jit(solution)/shard_map/pallas_call | solution.py:242
  30.6 1.8 %copy.5 = bf16[64,24,24,24]{0,3,2,1:T(8,128)(2,1)} copy(bf16[64,24,24,24]{0,3,2,1:T(8,128)(2,1)S(1)} %bitcast.3) | data formatting | bytes 3538944

commit v5 on v4

--- a/solution.py
+++ b/solution.py
@@ -216,6 +216,11 @@
             if n == max(0, (l - 1) * SLABS + X_END):
                 receive_x(l)
                 arrived.append((l, 0))
+        if n == (LAYERS - 2) * SLABS + max(end for _, _, _, end in GROUPS):
+            for l in range(LAYERS):
+                for i in range(len(GROUPS)):
+                    for c in copies(l, i):
+                        c.wait_send()
         for l in range(LAYERS):
             for j in range(1, SLABS):
                 if n - l * SLABS == READY[j]:
@@ -226,10 +231,6 @@
             fix(l, j)
         if n < LAYERS * SLABS:
             multiply(n // SLABS, ORDER[n % SLABS])
-    for l in range(LAYERS):
-        for i in range(len(GROUPS)):
-            for c in copies(l, i):
-                c.wait_send()
 
 
 def solution(mesh):

time: 32.5 us -> 32.5 us (level)
  no operation moved by 1% of the time
where the time goes in v5:
time: 32.5 us; the launch traced here: 32.4 us
  Pallas kernels  30.6 us (94%)
  local copies, waits for them, and re-layouts  1.8 us (6%)
    pallas_call x1, Pallas kernels, local(): pl.pallas_call(kernel, out_shape=pltpu.VMEM((N, N, N, CH), BF16), in_spec...  30.6 us
    unnamed x1, local copies, waits for them, and re-layouts  1.8 us

profile of v5, /device:TPU:0, one launch (start us, length us, event | category | flops | bytes accessed | tf_op | source)
XLA Modules:
  0.0 32.4 jit_solution(16341153604760490349)
XLA Ops:
  0.0 30.6 %shard_map.37 = bf16[24,24,24,64]{3,2,1,0:T(8,128)(2,1)S(1)} custom-call(bf16[24,24,24,64]{3,2,1,0:T(8,128)(2,1)} %bitcast.4, bf16[3,3,3,3,64,64]{5,4,3,2,1,0:T(8,128)(2,1)} %bitcast.5, f32[3,64]{1,0:T(4,128)} %bias_hbm.1), custom_call_target="tpu_custom_call" | custom-call | tf_op jit(solution)/shard_map/pallas_call | solution.py:243
  30.6 1.8 %copy.5 = bf16[64,24,24,24]{0,3,2,1:T(8,128)(2,1)} copy(bf16[64,24,24,24]{0,3,2,1:T(8,128)(2,1)S(1)} %bitcast.3) | data formatting | bytes 3538944
